TPU v7x, 32 devices: a whole 2x2x4 slice. The times are simulated.
32 devices in a mesh: dp: 8 (over z, y), mp: 4 (over x, core).
Axes of the slice: x: 2, y: 2, z: 4, core: 2. Of those that a mesh axis runs over, the one named last changes fastest.
Arguments:
- prefix_hidden: bfloat16 [32, 1024, 2048], P(('dp', 'mp')), may hold values from -6 to 6
- prefix_len: int32 [32], P('dp'), may hold values from 256 to 1024
- actions: float32 [32, 50, 32], P('dp'), may hold values from -6 to 6
- noise: float32 [32, 50, 32], P('dp'), may hold values from -6 to 6
- time_index: int32 [32], P('dp'), may hold values from 0 to 999
- prefix_gain: float32 [2048], replicated, may hold values from 0.25 to 1.75
- key_weight: bfloat16 [2048, 256], P('dp'), may hold values from -0.125 to 0.125
- value_weight: bfloat16 [2048, 256], P('dp'), may hold values from -0.125 to 0.125
- action_in: bfloat16 [32, 1024], replicated, may hold values from -1 to 1
- attn_gain: float32 [1024], replicated, may hold values from 0.25 to 1.75
- query_w: bfloat16 [1024, 2048], P('dp', 'mp'), may hold values from -0.1875 to 0.1875
- akey_w: bfloat16 [1024, 256], P('dp'), may hold values from -0.1875 to 0.1875
- avalue_w: bfloat16 [1024, 256], P('dp'), may hold values from -0.1875 to 0.1875
- out_w: bfloat16 [2048, 1024], P('mp', 'dp'), may hold values from -0.125 to 0.125
- mlp_gain: float32 [1024], replicated, may hold values from 0.25 to 1.75
- gate_w: bfloat16 [1024, 4096], P('dp', 'mp'), may hold values from -0.1875 to 0.1875
- up_w: bfloat16 [1024, 4096], P('dp', 'mp'), may hold values from -0.1875 to 0.1875
- down_w: bfloat16 [4096, 1024], P('mp', 'dp'), may hold values from -0.09375 to 0.09375
- final_gain: float32 [1024], replicated, may hold values from 0.25 to 1.75
- head_w: bfloat16 [1024, 32], replicated, may hold values from -0.1875 to 0.1875
Outputs:
- velocity: float32 [32, 50, 32], P(('dp', 'mp'))
- ep_loss: float32 [32], P(('dp', 'mp'))
Inputs may be any that keep to these rules, and one draw needn't show every extreme that they name: `prefix_len`: prefix positions at or above an episode's length are padding that no output reads.
All inputs are finite; a program needn't handle non-finite values.
Results may differ from a plain program's by a relative error of at most 0.009.
Values may be sent and summed in bfloat16 or wider, within the bound.
No kernel may reach another device: no remote copies, remote signals or barrier semaphores. Data moves between devices by JAX's collectives and lax.ppermute only.
A program may use at most 64 MiB of HBM per device.

v0:
```python
import math
import jax
import jax.numpy as jnp
from jax import lax
from jax.sharding import PartitionSpec as P

TSTEPS = 1000


def rms(values, gain):
    return values * lax.rsqrt(jnp.mean(values * values, axis=-1, keepdims=True) + 1e-06) * gain


def time_embed(times, width):
    half = width // 2
    steps = jnp.arange(half, dtype=jnp.float32)
    period = 0.004 * jnp.power(jnp.float32(1000.0), steps / (half - 1))
    angle = times[:, None] * (2.0 * math.pi) / period[None, :]
    return jnp.concatenate([jnp.sin(angle), jnp.cos(angle)], axis=-1)


def attend(query, pkeys, pvals, akeys, avals, lengths):
    live = jnp.arange(pkeys.shape[1], dtype=jnp.int32)[None, :] < lengths[:, None]
    scores = jnp.einsum("erd,epd->erp", query, pkeys, preferred_element_type=jnp.float32)
    probs = jnp.where(live[:, None, :], jnp.exp(scores), 0.0)
    action_scores = jnp.einsum("erd,ecd->erc", query, akeys, preferred_element_type=jnp.float32)
    action_probs = jnp.exp(action_scores)
    denom = jnp.sum(probs, axis=-1) + jnp.sum(action_probs, axis=-1)
    weighted = jnp.einsum(
        "erp,epd->erd", probs.astype(jnp.bfloat16), pvals, preferred_element_type=jnp.float32
    )
    weighted = weighted + jnp.einsum(
        "erc,ecd->erd", action_probs.astype(jnp.bfloat16), avals, preferred_element_type=jnp.float32
    )
    return (weighted / denom[:, :, None]).astype(jnp.bfloat16)


def on_device(
    prefix_hidden,
    prefix_len,
    actions,
    noise,
    time_index,
    prefix_gain,
    key_weight,
    value_weight,
    action_in,
    attn_gain,
    query_w,
    akey_w,
    avalue_w,
    out_w,
    mlp_gain,
    gate_w,
    up_w,
    down_w,
    final_gain,
    head_w,
):
    own_eps, positions, width = prefix_hidden.shape
    group_eps, span, adim = actions.shape
    expert = action_in.shape[1]
    head_size = key_weight.shape[1]
    local_heads = query_w.shape[1] // head_size
    rows_total = group_eps * span
    own_rows = own_eps * span
    member = lax.axis_index("mp")
    first_row = member * own_rows
    first_ep = member * own_eps
    times = (time_index.astype(jnp.float32) + 0.5) / TSTEPS
    x_t = times[:, None, None] * noise + (1.0 - times)[:, None, None] * actions
    target = noise - actions
    x_in = x_t.reshape(rows_total, adim).astype(jnp.bfloat16)
    temb = time_embed(times, expert)
    h0 = (
        jnp.dot(x_in, action_in, preferred_element_type=jnp.float32).reshape(
            group_eps, span, expert
        )
        + temb[:, None, :]
    )
    h0 = h0.reshape(rows_total, expert)
    key_full, value_full = (
        lax.all_gather(key_weight, "dp", axis=0, tiled=True),
        lax.all_gather(value_weight, "dp", axis=0, tiled=True),
    )
    prefix_normed = rms(
        prefix_hidden.reshape(own_eps * positions, width).astype(jnp.float32), prefix_gain
    ).astype(jnp.bfloat16)
    pkeys = (
        jnp.dot(prefix_normed, key_full, preferred_element_type=jnp.float32)
        .astype(jnp.bfloat16)
        .reshape(own_eps, positions, head_size)
    )
    pvals = (
        jnp.dot(prefix_normed, value_full, preferred_element_type=jnp.float32)
        .astype(jnp.bfloat16)
        .reshape(own_eps, positions, head_size)
    )
    normed = rms(h0, attn_gain).astype(jnp.bfloat16)
    query_full, akey_full, avalue_full = (
        lax.all_gather(query_w, "dp", axis=0, tiled=True),
        lax.all_gather(akey_w, "dp", axis=0, tiled=True),
        lax.all_gather(avalue_w, "dp", axis=0, tiled=True),
    )
    query = (
        jnp.dot(normed, query_full, preferred_element_type=jnp.float32) * head_size ** (-0.5)
    ).astype(jnp.bfloat16)
    akeys = (
        jnp.dot(normed, akey_full, preferred_element_type=jnp.float32)
        .astype(jnp.bfloat16)
        .reshape(group_eps, span, head_size)
    )
    avals = (
        jnp.dot(normed, avalue_full, preferred_element_type=jnp.float32)
        .astype(jnp.bfloat16)
        .reshape(group_eps, span, head_size)
    )
    keys_all, vals_all = (
        lax.all_gather(pkeys, "mp", axis=0, tiled=True),
        lax.all_gather(pvals, "mp", axis=0, tiled=True),
    )
    attn = attend(
        query.reshape(group_eps, span * local_heads, head_size),
        keys_all,
        vals_all,
        akeys,
        avals,
        prefix_len,
    )
    attn = attn.reshape(rows_total, local_heads * head_size)
    out_full = lax.all_gather(out_w, "dp", axis=1, tiled=True)
    gate_full, up_full = (
        lax.all_gather(gate_w, "dp", axis=0, tiled=True),
        lax.all_gather(up_w, "dp", axis=0, tiled=True),
    )
    down_full = lax.all_gather(down_w, "dp", axis=1, tiled=True)
    h0_own = lax.dynamic_slice_in_dim(h0, first_row, own_rows, 0)
    h1 = h0_own + lax.psum_scatter(
        jnp.dot(attn, out_full, preferred_element_type=jnp.float32).astype(jnp.bfloat16),
        "mp",
        scatter_dimension=0,
        tiled=True,
    ).astype(jnp.float32)
    mixed_own = rms(h1, mlp_gain).astype(jnp.bfloat16)
    mixed = lax.all_gather(mixed_own, "mp", axis=0, tiled=True)
    gate = jnp.dot(mixed, gate_full, preferred_element_type=jnp.float32)
    upper = jnp.dot(mixed, up_full, preferred_element_type=jnp.float32)
    hidden = (jax.nn.gelu(gate, approximate=True) * upper).astype(jnp.bfloat16)
    h2 = h1 + lax.psum_scatter(
        jnp.dot(hidden, down_full, preferred_element_type=jnp.float32).astype(jnp.bfloat16),
        "mp",
        scatter_dimension=0,
        tiled=True,
    ).astype(jnp.float32)
    final = rms(h2, final_gain).astype(jnp.bfloat16)
    velocity = jnp.dot(final, head_w, preferred_element_type=jnp.float32).reshape(
        own_eps, span, adim
    )
    own_target = lax.dynamic_slice_in_dim(target, first_ep, own_eps, 0)
    diff = velocity - own_target
    ep_loss = jnp.mean(diff * diff, axis=(1, 2))
    return (velocity, ep_loss)


def solution(mesh):
    in_specs = (
        P(("dp", "mp"), None, None),
        P("dp"),
        P("dp", None, None),
        P("dp", None, None),
        P("dp"),
        P(),
        P("dp", None),
        P("dp", None),
        P(),
        P(),
        P("dp", "mp"),
        P("dp", None),
        P("dp", None),
        P("mp", "dp"),
        P(),
        P("dp", "mp"),
        P("dp", "mp"),
        P("mp", "dp"),
        P(),
        P(),
    )
    out_specs = (P(("dp", "mp"), None, None), P(("dp", "mp")))
    return jax.shard_map(
        on_device, mesh=mesh, in_specs=in_specs, out_specs=out_specs, check_vma=False
    )
```

profile of v0, /device:TPU:6, one launch (start us, length us, event | category | flops | bytes accessed | tf_op | source)
XLA Modules:
  0.0 404.9 jit_solution(4263375516487390356)
XLA Ops:
  7.2 0.0 all-gather.15.cloned.1.call-start
  7.2 0.7 all-gather.15.cloned.1.call-update
  7.9 0.0 all-gather.17.cloned.1.call-start
  8.0 0.7 all-gather.17.cloned.1.call-update
  8.7 0.0 all-gather.13.cloned.1.call-start
  8.7 0.7 all-gather.13.cloned.1.call-update
  9.4 0.0 all-gather.27.cloned.1.call-start
  9.5 3.1 fusion.2
  12.5 38.1 %all-gather.15.cloned.1.call-done = bf16[2048,256]{1,0:T(8,128)(2,1)} async-done(((bf16[256,256]{1,0:T(8,128)(2,1)}), bf16[2048,256]{1,0:T(8,128)(2,1)}) %all-gather.15.cloned.1.call-update) | async-done | bytes 1048592 | tf_op jit(solution)/shard_map/all_gather | solution.py:83
  50.7 4.6 %convolution_convert_fusion.1 = bf16[1024,256]{1,0:T(8,128)(2,1)} fusion(bf16[2048,256]{1,0:T(8,128)(2,1)} %all-gather.15.cloned.1.call-done, bf16[1,1024,2048]{2,1,0:T(8,128)(2,1)} %param.20, f32[2048]{0:T(1024)S(1)} %copy-done.12, f32[1024]{0:T(1024)S(1)} %add_rsqrt_fusion), kind=kOutput, calls=%fused_computation.9 | convolution fusion | flops 1082392576 | bytes 5779456 | tf_op jit(solution)/shard_map/dot_general | solution.py:90
  55.3 0.0 all-gather.27.cloned.1.call-update
  55.4 0.0 all-gather.29.cloned.1.call-start
  55.4 36.4 %all-gather.17.cloned.1.call-done = bf16[2048,256]{1,0:T(8,128)(2,1)} async-done(((bf16[256,256]{1,0:T(8,128)(2,1)}), bf16[2048,256]{1,0:T(8,128)(2,1)}) %all-gather.17.cloned.1.call-update) | async-done | bytes 1048592 | tf_op jit(solution)/shard_map/all_gather | solution.py:84
  91.8 4.6 %convolution_convert_fusion = bf16[1024,256]{1,0:T(8,128)(2,1)} fusion(bf16[2048,256]{1,0:T(8,128)(2,1)} %all-gather.17.cloned.1.call-done, bf16[1,1024,2048]{2,1,0:T(8,128)(2,1)} %param.20, f32[2048]{0:T(1024)S(1)} %copy-done.12, f32[1024]{0:T(1024)S(1)} %add_rsqrt_fusion), kind=kOutput, calls=%fused_computation.8 | convolution fusion | flops 1082392576 | bytes 5779456 | tf_op jit(solution)/shard_map/dot_general | solution.py:95
  96.4 0.0 all-gather.29.cloned.1.call-update
  96.5 0.0 all-gather.19.cloned.1.call-start
  96.5 0.5 all-gather.19.cloned.1.call-update
  97.0 0.0 all-gather.21.cloned.1.call-start
  97.1 0.7 all-gather.21.cloned.1.call-update
  97.8 0.0 all-gather.23.cloned.1.call-start
  97.8 0.7 all-gather.23.cloned.1.call-update
  98.5 0.0 all-gather.25.cloned.1.call-start
  98.6 0.7 all-gather.25.cloned.1.call-update
  99.3 0.1 fusion.38
  99.5 0.5 multiply_reduce_fusion
  100.0 0.1 reshape.115
  100.1 0.1 rsqrt.36
  100.2 30.9 %all_gather.41 = bf16[1024,256]{1,0:T(8,128)(2,1)S(1)} all-gather(bf16[128,256]{1,0:T(8,128)(2,1)S(1)} %copy-done.3), channel_id=1, replica_groups=mesh['dp'=8,'mp'=4] {'dp'}, dimensions={0}, use_global_device_ids=true | all-gather | bytes 589824 | tf_op jit(solution)/shard_map/all_gather | solution.py:102
  131.1 0.1 multiply_convert_fusion
  131.2 0.3 convolution_convert_fusion.5
  131.6 31.5 %all_gather.42 = bf16[1024,256]{1,0:T(8,128)(2,1)S(1)} all-gather(bf16[128,256]{1,0:T(8,128)(2,1)S(1)} %copy-done.4), channel_id=1, replica_groups=mesh['dp'=8,'mp'=4] {'dp'}, dimensions={0}, use_global_device_ids=true | all-gather | bytes 589824 | tf_op jit(solution)/shard_map/all_gather | solution.py:103
  163.1 0.3 convolution_convert_fusion.4
  163.5 0.1 iota_compare_fusion
  163.5 1.6 fusion.10
  165.1 0.1 reshape.116
  165.2 0.2 fusion.46
  165.5 0.0 all-gather.27.cloned.1.call-done
  165.5 2.5 fusion.45
  168.0 14.4 %all-gather.29.cloned.1.call-done = bf16[4096,256]{1,0:T(8,128)(2,1)} async-done(((bf16[1024,256]{1,0:T(8,128)(2,1)}), bf16[4096,256]{1,0:T(8,128)(2,1)}) %all-gather.29.cloned.1.call-update) | async-done | bytes 2097168 | tf_op jit(solution)/shard_map/all_gather | solution.py:120
  182.4 2.0 fusion.11
  184.5 0.3 fusion.9
  184.7 0.1 reshape.121
  184.8 39.4 %all-gather.19.cloned.1.call-done = bf16[512,1024]{1,0:T(8,128)(2,1)} async-done(((bf16[512,128]{1,0:T(8,128)(2,1)}), bf16[512,1024]{1,0:T(8,128)(2,1)}) %all-gather.19.cloned.1.call-update) | async-done | bytes 1048592 | tf_op jit(solution)/shard_map/all_gather | solution.py:131
  224.2 1.6 convolution_convert_fusion.3
  225.8 10.1 %fusion = bf16[56,1024]{1,0:T(8,128)(2,1)S(1)} fusion(bf16[200,1024]{1,0:T(8,128)(2,1)S(1)} %convolution_convert_fusion.3), kind=kCustom, calls=%all-reduce-scatter | all-reduce-scatter fusion | flops 229377 | bytes 524800
  236.0 1.9 collective-permute-start
  237.9 0.6 dynamic-slice.6
  239.1 2.2 collective-permute-done
  241.4 0.2 concatenate.4
  241.6 0.2 multiply_reduce_fusion.2
  241.8 0.1 fusion.25
  241.9 6.3 %all-gather.2 = bf16[4,50,1024]{2,1,0:T(8,128)(2,1)S(1)} all-gather(bf16[1,50,1024]{2,1,0:T(8,128)(2,1)S(1)} %fusion.25), channel_id=1, replica_groups=mesh['dp'=8,'mp'=4] {'mp'}, dimensions={0}, use_global_device_ids=true | all-gather | bytes 512000 | tf_op jit(solution)/shard_map/all_gather | solution.py:145
  248.2 0.1 reshape.127
  248.3 25.8 %all-gather.21.cloned.1.call-done = bf16[1024,1024]{1,0:T(8,128)(2,1)} async-done(((bf16[128,1024]{1,0:T(8,128)(2,1)}), bf16[1024,1024]{1,0:T(8,128)(2,1)}) %all-gather.21.cloned.1.call-update) | async-done | bytes 2097168 | tf_op jit(solution)/shard_map/all_gather | solution.py:133
  274.1 2.2 fusion.47
  276.3 47.6 %all-gather.23.cloned.1.call-done = bf16[1024,1024]{1,0:T(8,128)(2,1)} async-done(((bf16[128,1024]{1,0:T(8,128)(2,1)}), bf16[1024,1024]{1,0:T(8,128)(2,1)}) %all-gather.23.cloned.1.call-update) | async-done | bytes 2097168 | tf_op jit(solution)/shard_map/all_gather | solution.py:134
  323.8 51.9 %all-gather.25.cloned.1.call-done = bf16[1024,1024]{1,0:T(8,128)(2,1)} async-done(((bf16[1024,128]{1,0:T(8,128)(2,1)}), bf16[1024,1024]{1,0:T(8,128)(2,1)}) %all-gather.25.cloned.1.call-update) | async-done | bytes 2097168 | tf_op jit(solution)/shard_map/all_gather | solution.py:136
  375.7 3.3 convolution_convert_fusion.2
  379.0 10.2 %fusion.1 = bf16[56,1024]{1,0:T(8,128)(2,1)S(1)} fusion(bf16[200,1024]{1,0:T(8,128)(2,1)S(1)} %convolution_convert_fusion.2), kind=kCustom, calls=%all-reduce-scatter.1 | all-reduce-scatter fusion | flops 229377 | bytes 524800
  389.3 1.9 collective-permute-start.1
  391.2 3.5 collective-permute-done.1
  394.7 0.2 concatenate.5
  394.9 0.2 multiply_reduce_fusion.1
  395.1 1.5 fusion.35
  (39 shorter events, 0.2 us)
Async XLA Ops:
  7.2 92.3 %copy-start = (bf16[32,1024]{1,0:T(8,128)(2,1)S(1)}, bf16[32,1024]{1,0:T(8,128)(2,1)}, u32[]{:S(2)}) copy-start(bf16[32,1024]{1,0:T(8,128)(2,1)} %param.28) | copy-start | bytes 196612
  7.2 43.5 %all-gather.15.cloned.1.call-start = ((), (), s32[]{:S(2)}) async-start(), calls=%async_computation.1 | async-start | bytes 1179648 | tf_op jit(solution)/shard_map/all_gather | solution.py:83
  7.9 83.9 %all-gather.17.cloned.1.call-start = ((), (), s32[]{:S(2)}) async-start(), calls=%async_computation.2 | async-start | bytes 1179648 | tf_op jit(solution)/shard_map/all_gather | solution.py:84
  8.7 154.9 %all-gather.13.cloned.1.call-start = ((), (), s32[]{:S(2)}) async-start(), calls=%async_computation | async-start | bytes 1179648 | tf_op jit(solution)/shard_map/all_gather | solution.py:101
  9.4 41.3 %copy-start.12 = (f32[2048]{0:T(1024)S(1)}, f32[2048]{0:T(1024)}, u32[]{:S(2)}) copy-start(f32[2048]{0:T(1024)} %param.25) | copy-start | bytes 24580
  9.4 156.1 %all-gather.27.cloned.1.call-start = ((), (), s32[]{:S(2)}) async-start(), calls=%async_computation.7 | async-start | bytes 2621440 | tf_op jit(solution)/shard_map/all_gather | solution.py:119
  55.4 43.9 %copy-start.11 = (s32[4]{0:T(128)S(1)}, s32[4]{0:T(128)}, u32[]{:S(2)}) copy-start(s32[4]{0:T(128)} %param.24) | copy-start | bytes 52
  55.4 44.1 %copy-start.1 = (f32[4,50,32]{1,2,0:T(8,128)S(1)}, f32[4,50,32]{1,2,0:T(8,128)}, u32[]{:S(2)}) copy-start(f32[4,50,32]{1,2,0:T(8,128)} %param.22) | copy-start | bytes 76804
  55.4 44.1 %copy-start.2 = (f32[4,50,32]{1,2,0:T(8,128)S(1)}, f32[4,50,32]{1,2,0:T(8,128)}, u32[]{:S(2)}) copy-start(f32[4,50,32]{1,2,0:T(8,128)} %param.23) | copy-start | bytes 76804
  55.4 127.0 %all-gather.29.cloned.1.call-start = ((), (), s32[]{:S(2)}) async-start(), calls=%async_computation.8 | async-start | bytes 2621440 | tf_op jit(solution)/shard_map/all_gather | solution.py:120
  96.4 3.8 copy-start.3
  96.5 127.8 %all-gather.19.cloned.1.call-start = ((), (), s32[]{:S(2)}) async-start(), calls=%async_computation.3 | async-start | bytes 1179648 | tf_op jit(solution)/shard_map/all_gather | solution.py:131
  97.0 34.1 %copy-start.6 = (f32[1024]{0:T(1024)S(1)}, f32[1024]{0:T(1024)}, u32[]{:S(2)}) copy-start(f32[1024]{0:T(1024)} %param.29) | copy-start | bytes 12292
  97.0 177.0 %all-gather.21.cloned.1.call-start = ((), (), s32[]{:S(2)}) async-start(), calls=%async_computation.4 | async-start | bytes 2359296 | tf_op jit(solution)/shard_map/all_gather | solution.py:133
  97.8 226.0 %all-gather.23.cloned.1.call-start = ((), (), s32[]{:S(2)}) async-start(), calls=%async_computation.5 | async-start | bytes 2359296 | tf_op jit(solution)/shard_map/all_gather | solution.py:134
  98.5 277.1 %all-gather.25.cloned.1.call-start = ((), (), s32[]{:S(2)}) async-start(), calls=%async_computation.6 | async-start | bytes 2359296 | tf_op jit(solution)/shard_map/all_gather | solution.py:136
  100.0 31.6 %copy-start.4 = (bf16[128,256]{1,0:T(8,128)(2,1)S(1)}, bf16[128,256]{1,0:T(8,128)(2,1)}, u32[]{:S(2)}) copy-start(bf16[128,256]{1,0:T(8,128)(2,1)} %param.32) | copy-start | bytes 196612
  131.1 32.4 %copy-start.9 = (s32[4]{0:T(128)S(1)}, s32[4]{0:T(128)}, u32[]{:S(2)}) copy-start(s32[4]{0:T(128)} %param.21) | copy-start | bytes 52
  184.5 53.4 %copy-start.10 = (u32[32]{0:T(128)S(1)}, u32[32]{0:T(128)}, u32[]{:S(2)}) copy-start(u32[32]{0:T(128)} %constant.63) | copy-start | bytes 388
  184.7 57.0 %copy-start.7 = (f32[1024]{0:T(1024)S(1)}, f32[1024]{0:T(1024)}, u32[]{:S(2)}) copy-start(f32[1024]{0:T(1024)} %param.34) | copy-start | bytes 12292
  236.0 5.4 %collective-permute-start = (bf16[18,1024]{1,0:T(8,128)(2,1)S(1)}, bf16[18,1024]{1,0:T(8,128)(2,1)S(1)}, u32[]{:S(2)}, u32[]{:S(2)}) collective-permute-start(bf16[18,1024]{1,0:T(8,128)(2,1)S(1)} %slice), channel_id=1, source_target_pairs={{0,1},{1,2},{2,3},{4,5},{5,6},{6,7},{8,9},{9,10},{10,11},{12,13},{... | collective-permute-start | bytes 110600
  276.2 118.9 %copy-start.5 = (bf16[1024,32]{0,1:T(8,128)(2,1)S(1)}, bf16[1024,32]{0,1:T(8,128)(2,1)}, u32[]{:S(2)}) copy-start(bf16[1024,32]{0,1:T(8,128)(2,1)} %param.39) | copy-start | bytes 196612
  276.3 118.9 %copy-start.8 = (f32[1024]{0:T(1024)S(1)}, f32[1024]{0:T(1024)}, u32[]{:S(2)}) copy-start(f32[1024]{0:T(1024)} %param.38) | copy-start | bytes 12292
  389.3 5.4 %collective-permute-start.1 = (bf16[18,1024]{1,0:T(8,128)(2,1)S(1)}, bf16[18,1024]{1,0:T(8,128)(2,1)S(1)}, u32[]{:S(2)}, u32[]{:S(2)}) collective-permute-start(bf16[18,1024]{1,0:T(8,128)(2,1)S(1)} %slice.1), channel_id=1, source_target_pairs={{0,1},{1,2},{2,3},{4,5},{5,6},{6,7},{8,9},{9,10},{10,11},{12,13},{... | collective-permute-start | bytes 110600
Sparse Core Ops, SparseCore 0:
  10.1 40.5 all-gather.14
  52.8 38.9 all-gather.16
  94.0 41.6 all-gather.12
  137.0 21.2 all-gather.26
  159.8 22.5 all-gather.28
  184.3 39.8 all-gather.18
  226.3 47.6 all-gather.20
  276.2 47.6 all-gather.22
  325.9 49.7 all-gather.24
where the time goes:
time: 405 us
  waiting for transfers between devices  264 us (65%)
  blocking collectives  89.1 us (22%)
  matrix products  25.5 us (6%)
  between operations  16.7 us (4%)
  starting transfers between devices  4.19 us (1%)
    all_gather x1, waiting for transfers between devices, on_device(): down_full = lax.all_gather(down_w, 'dp', axis=1, tiled=True)  51.9 us
    all_gather x1, waiting for transfers between devices, on_device(): lax.all_gather(up_w, 'dp', axis=0, tiled=True)  47.6 us
    all_gather x1, waiting for transfers between devices, on_device(): out_full = lax.all_gather(out_w, 'dp', axis=1, tiled=True)  39.4 us
    all_gather x1, waiting for transfers between devices, on_device(): lax.all_gather(key_weight, 'dp', axis=0, tiled=True)  38.1 us
    all_gather x1, waiting for transfers between devices, on_device(): lax.all_gather(value_weight, 'dp', axis=0, tiled=True)  36.4 us
    all_gather x1, blocking collectives, on_device(): lax.all_gather(avalue_w, 'dp', axis=0, tiled=True)  31.5 us
    all_gather x1, blocking collectives, on_device(): lax.all_gather(akey_w, 'dp', axis=0, tiled=True)  30.9 us
    all_gather x1, waiting for transfers between devices, on_device(): lax.all_gather(gate_w, 'dp', axis=0, tiled=True)  25.8 us
  transfers between devices with their start and end apart: 11, of which 9 were waited for; matrix products, arithmetic and copies ran while one was open for 9% of the time, Pallas kernels for 0%

commit v1 on v0

--- a/solution.py
+++ b/solution.py
@@ -133,7 +133,12 @@
         lax.all_gather(gate_w, "dp", axis=0, tiled=True),
         lax.all_gather(up_w, "dp", axis=0, tiled=True),
     )
-    down_full = lax.all_gather(down_w, "dp", axis=1, tiled=True)
+    ring = [down_w]
+    for hop in range(7):
+        ring.append(lax.ppermute(ring[-1], "dp", [(dev, (dev + 1) % 8) for dev in range(8)]))
+    down_full = jnp.roll(
+        jnp.concatenate(ring[::-1], axis=1), (lax.axis_index("dp") + 1) * ring[0].shape[1], axis=1
+    )
     h0_own = lax.dynamic_slice_in_dim(h0, first_row, own_rows, 0)
     h1 = h0_own + lax.psum_scatter(
         jnp.dot(attn, out_full, preferred_element_type=jnp.float32).astype(jnp.bfloat16),

time: 405 us -> 361 us (0.89)
  waiting for transfers between devices: 264 us -> 178 us
  starting transfers between devices: 4.19 us -> 22.2 us
  local copies, waits for them, and re-layouts: 1.63 us -> 18.1 us
  blocking collectives: 89.1 us -> 93.4 us
    all_gather x1 -> x0, waiting for transfers between devices: 51.9 us -> none  [on_device(): down_full = lax.all_gather(down_w, 'dp', axis=1, tiled=True)]
    all_gather x1, waiting for transfers between devices: 39.4 us -> 0.02 us  [on_device(): out_full = lax.all_gather(out_w, 'dp', axis=1, tiled=True)]
    ppermute x0 -> x7, waiting for transfers between devices: none -> 27.3 us  [on_device(): lax.ppermute(ring[-1], 'dp', [(dev, (dev + 1) % 8) for dev in range(8)])]
    ppermute x0 -> x7, starting transfers between devices: none -> 18.1 us  [on_device(): lax.ppermute(ring[-1], 'dp', [(dev, (dev + 1) % 8) for dev in range(8)])]
    unnamed x32 -> x53, local copies, waits for them, and re-layouts: 1.19 us -> 16.3 us
    all_gather x1, waiting for transfers between devices: 14.4 us -> 0.02 us  [on_device(): lax.all_gather(pvals, 'mp', axis=0, tiled=True)]
    all_gather x1, waiting for transfers between devices: 25.8 us -> 19.5 us  [on_device(): lax.all_gather(gate_w, 'dp', axis=0, tiled=True)]
    unnamed x11 -> x10, waiting for transfers between devices: 10.4 us -> 9.51 us
  transfers between devices with their start and end apart: 11 -> 17, of which waited for: 9 -> 11; matrix products, arithmetic and copies ran while one was open for 9% -> 14% of each run, Pallas kernels for 0% -> 0%
where the time goes in v1:
time: 361 us; the launch traced here: 359 us
  waiting for transfers between devices  178 us (49%)
  blocking collectives  93.4 us (26%)
  matrix products  26.2 us (7%)
  starting transfers between devices  22.2 us (6%)
  local copies, waits for them, and re-layouts  18.1 us (5%)
  between operations  17 us (5%)
  other arithmetic  3.95 us (1%)
    all_gather x1, waiting for transfers between devices, on_device(): lax.all_gather(up_w, 'dp', axis=0, tiled=True)  47.6 us
    all_gather x1, waiting for transfers between devices, on_device(): lax.all_gather(key_weight, 'dp', axis=0, tiled=True)  38.1 us
    all_gather x1, waiting for transfers between devices, on_device(): lax.all_gather(value_weight, 'dp', axis=0, tiled=True)  36.4 us
    all_gather x1, blocking collectives, on_device(): lax.all_gather(akey_w, 'dp', axis=0, tiled=True)  34.3 us
    all_gather x1, blocking collectives, on_device(): lax.all_gather(avalue_w, 'dp', axis=0, tiled=True)  34.1 us
    ppermute x7, waiting for transfers between devices, on_device(): lax.ppermute(ring[-1], 'dp', [(dev, (dev + 1) % 8) for dev in range(8)])  27.3 us
    all_gather x1, waiting for transfers between devices, on_device(): lax.all_gather(gate_w, 'dp', axis=0, tiled=True)  19.5 us
    unnamed x2, blocking collectives  18.6 us
  transfers between devices with their start and end apart: 17, of which 11 were waited for; matrix products, arithmetic and copies ran while one was open for 14% of the time, Pallas kernels for 0%

profile of v1, /device:TPU:6, one launch (start us, length us, event | category | flops | bytes accessed | tf_op | source)
XLA Modules:
  0.0 359.4 jit_solution(6073681266011720273)
XLA Ops:
  7.2 0.7 all-gather.14.cloned.1.call-update
  8.0 0.7 all-gather.16.cloned.1.call-update
  8.7 0.7 all-gather.12.cloned.1.call-update
  9.5 3.1 fusion.2
  12.5 38.1 %all-gather.14.cloned.1.call-done = bf16[2048,256]{1,0:T(8,128)(2,1)} async-done(((bf16[256,256]{1,0:T(8,128)(2,1)}), bf16[2048,256]{1,0:T(8,128)(2,1)}) %all-gather.14.cloned.1.call-update) | async-done | bytes 1048592 | tf_op jit(solution)/shard_map/all_gather | solution.py:83
  50.7 4.6 %convolution_convert_fusion.1 = bf16[1024,256]{1,0:T(8,128)(2,1)} fusion(bf16[2048,256]{1,0:T(8,128)(2,1)} %all-gather.14.cloned.1.call-done, bf16[1,1024,2048]{2,1,0:T(8,128)(2,1)} %param.20, f32[2048]{0:T(1024)S(1)} %copy-done.15, f32[1024]{0:T(1024)S(1)} %add_rsqrt_fusion), kind=kOutput, calls=%fused_computation.11 | convolution fusion | flops 1082392576 | bytes 5779456 | tf_op jit(solution)/shard_map/dot_general | solution.py:90
  55.4 36.4 %all-gather.16.cloned.1.call-done = bf16[2048,256]{1,0:T(8,128)(2,1)} async-done(((bf16[256,256]{1,0:T(8,128)(2,1)}), bf16[2048,256]{1,0:T(8,128)(2,1)}) %all-gather.16.cloned.1.call-update) | async-done | bytes 1048592 | tf_op jit(solution)/shard_map/all_gather | solution.py:84
  91.8 4.6 %convolution_convert_fusion = bf16[1024,256]{1,0:T(8,128)(2,1)} fusion(bf16[2048,256]{1,0:T(8,128)(2,1)} %all-gather.16.cloned.1.call-done, bf16[1,1024,2048]{2,1,0:T(8,128)(2,1)} %param.20, f32[2048]{0:T(1024)S(1)} %copy-done.15, f32[1024]{0:T(1024)S(1)} %add_rsqrt_fusion), kind=kOutput, calls=%fused_computation.10 | convolution fusion | flops 1082392576 | bytes 5779456 | tf_op jit(solution)/shard_map/dot_general | solution.py:95
  96.5 0.5 all-gather.18.cloned.1.call-update
  97.1 0.7 all-gather.20.cloned.1.call-update
  97.9 1.3 collective-permute-start
  99.2 6.5 %collective-permute-done = bf16[1024,128]{1,0:T(8,128)(2,1)S(1)} collective-permute-done((bf16[1024,128]{1,0:T(8,128)(2,1)S(1)}, bf16[1024,128]{1,0:T(8,128)(2,1)S(1)}, u32[]{:S(2)}, u32[]{:S(2)}) %collective-permute-start) | collective-permute-done | bytes 262176 | tf_op jit(solution)/shard_map/ppermute | solution.py:138
  105.7 3.1 collective-permute-start.1
  108.8 5.5 %collective-permute-done.1 = bf16[1024,128]{1,0:T(8,128)(2,1)S(1)} collective-permute-done((bf16[1024,128]{1,0:T(8,128)(2,1)S(1)}, bf16[1024,128]{1,0:T(8,128)(2,1)S(1)}, u32[]{:S(2)}, u32[]{:S(2)}) %collective-permute-start.1) | collective-permute-done | bytes 262176 | tf_op jit(solution)/shard_map/ppermute | solution.py:138
  114.4 3.4 collective-permute-start.2
  117.9 34.1 %all_gather.39 = bf16[1024,256]{1,0:T(8,128)(2,1)S(1)} all-gather(bf16[128,256]{1,0:T(8,128)(2,1)S(1)} %copy-done.7), channel_id=1, replica_groups=mesh['dp'=8,'mp'=4] {'dp'}, dimensions={0}, use_global_device_ids=true | all-gather | bytes 589824 | tf_op jit(solution)/shard_map/all_gather | solution.py:103
  152.1 3.3 collective-permute-start.3
  155.4 0.5 multiply_reduce_fusion
  155.8 5.8 %collective-permute-done.3 = bf16[1024,128]{1,0:T(8,128)(2,1)} collective-permute-done((bf16[1024,128]{1,0:T(8,128)(2,1)S(1)}, bf16[1024,128]{1,0:T(8,128)(2,1)}, u32[]{:S(2)}, u32[]{:S(2)}) %collective-permute-start.3) | collective-permute-done | bytes 262176 | tf_op jit(solution)/shard_map/ppermute | solution.py:138
  161.6 3.5 collective-permute-start.4
  165.5 5.5 %collective-permute-done.4 = bf16[1024,128]{1,0:T(8,128)(2,1)} collective-permute-done((bf16[1024,128]{1,0:T(8,128)(2,1)}, bf16[1024,128]{1,0:T(8,128)(2,1)}, u32[]{:S(2)}, u32[]{:S(2)}) %collective-permute-start.4) | collective-permute-done | bytes 262176 | tf_op jit(solution)/shard_map/ppermute | solution.py:138
  171.0 2.2 collective-permute-start.5
  173.2 34.3 %all_gather.38 = bf16[1024,256]{1,0:T(8,128)(2,1)S(1)} all-gather(bf16[128,256]{1,0:T(8,128)(2,1)} %param.31), channel_id=1, replica_groups=mesh['dp'=8,'mp'=4] {'dp'}, dimensions={0}, use_global_device_ids=true | all-gather | bytes 589824 | tf_op jit(solution)/shard_map/all_gather | solution.py:102
  207.5 0.3 convolution_convert_fusion.3
  207.8 1.3 collective-permute-start.6
  209.1 0.3 convolution_convert_fusion.4
  209.4 0.7 reshape.120
  210.1 0.6 dynamic-slice.6
  211.5 4.0 %collective-permute-done.6 = bf16[1024,128]{1,0:T(8,128)(2,1)S(1)} collective-permute-done((bf16[1024,128]{1,0:T(8,128)(2,1)S(1)}, bf16[1024,128]{1,0:T(8,128)(2,1)S(1)}, u32[]{:S(2)}, u32[]{:S(2)}) %collective-permute-start.6) | collective-permute-done | bytes 262176 | tf_op jit(solution)/shard_map/ppermute | solution.py:138
  215.5 0.7 constant_dynamic-update-slice_fusion.15
  216.2 0.7 constant_dynamic-update-slice_fusion.14
  216.9 1.7 constant_dynamic-update-slice_fusion.13
  218.7 1.7 constant_dynamic-update-slice_fusion.12
  220.4 0.8 constant_dynamic-update-slice_fusion.11
  221.1 0.7 constant_dynamic-update-slice_fusion.10
  221.9 0.7 constant_dynamic-update-slice_fusion.9
  222.6 0.7 constant_dynamic-update-slice_fusion.8
  223.3 1.6 fusion.15
  225.1 0.7 constant_dynamic-update-slice_fusion.7
  225.8 0.8 constant_dynamic-update-slice_fusion.6
  226.6 1.7 constant_dynamic-update-slice_fusion.5
  228.3 1.7 constant_dynamic-update-slice_fusion.4
  230.0 0.7 constant_dynamic-update-slice_fusion.3
  230.7 0.8 constant_dynamic-update-slice_fusion.2
  231.5 0.8 constant_dynamic-update-slice_fusion.1
  232.2 0.2 fusion.52
  232.5 2.5 fusion.51
  235.0 2.1 fusion.16
  237.1 0.3 fusion.14
  237.5 1.6 convolution_convert_fusion.2
  239.1 9.4 %fusion = bf16[56,1024]{1,0:T(8,128)(2,1)S(1)} fusion(bf16[200,1024]{1,0:T(8,128)(2,1)S(1)} %convolution_convert_fusion.2), kind=kCustom, calls=%all-reduce-scatter | all-reduce-scatter fusion | flops 229377 | bytes 524800
  248.5 1.9 collective-permute-start.7
  250.4 0.8 constant_dynamic-update-slice_fusion
  251.2 2.7 collective-permute-done.7
  254.4 6.3 %all-gather.2 = bf16[4,50,1024]{2,1,0:T(8,128)(2,1)S(1)} all-gather(bf16[1,50,1024]{2,1,0:T(8,128)(2,1)S(1)} %fusion.30), channel_id=1, replica_groups=mesh['dp'=8,'mp'=4] {'mp'}, dimensions={0}, use_global_device_ids=true | all-gather | bytes 512000 | tf_op jit(solution)/shard_map/all_gather | solution.py:150
  260.8 19.5 %all-gather.20.cloned.1.call-done = bf16[1024,1024]{1,0:T(8,128)(2,1)} async-done(((bf16[128,1024]{1,0:T(8,128)(2,1)}), bf16[1024,1024]{1,0:T(8,128)(2,1)}) %all-gather.20.cloned.1.call-update) | async-done | bytes 2097168 | tf_op jit(solution)/shard_map/all_gather | solution.py:133
  280.3 2.2 fusion.53
  282.5 47.6 %all-gather.22.cloned.1.call-done = bf16[1024,1024]{1,0:T(8,128)(2,1)} async-done(((bf16[128,1024]{1,0:T(8,128)(2,1)}), bf16[1024,1024]{1,0:T(8,128)(2,1)}) %all-gather.22.cloned.1.call-update) | async-done | bytes 2097168 | tf_op jit(solution)/shard_map/all_gather | solution.py:134
  330.1 3.3 fusion.8
  333.4 9.3 %fusion.1 = bf16[56,1024]{1,0:T(8,128)(2,1)S(1)} fusion(bf16[200,1024]{1,0:T(8,128)(2,1)S(1)} %fusion.8), kind=kCustom, calls=%all-reduce-scatter.1 | all-reduce-scatter fusion | flops 229377 | bytes 524800
  342.7 1.9 collective-permute-start.8
  344.7 3.5 collective-permute-done.8
  348.3 0.2 multiply_reduce_fusion.1
  348.6 2.2 fusion.40
  (72 shorter events, 2.1 us)
Async XLA Ops:
  7.2 148.2 %copy-start = (bf16[32,1024]{1,0:T(8,128)(2,1)S(1)}, bf16[32,1024]{1,0:T(8,128)(2,1)}, u32[]{:S(2)}) copy-start(bf16[32,1024]{1,0:T(8,128)(2,1)} %param.28) | copy-start | bytes 196612
  7.2 43.5 %copy-start.15 = (f32[2048]{0:T(1024)S(1)}, f32[2048]{0:T(1024)}, u32[]{:S(2)}) copy-start(f32[2048]{0:T(1024)} %param.25) | copy-start | bytes 24580
  7.2 43.5 %all-gather.14.cloned.1.call-start = ((), (), s32[]{:S(2)}) async-start(), calls=%async_computation.1 | async-start | bytes 1179648 | tf_op jit(solution)/shard_map/all_gather | solution.py:83
  7.9 83.9 %all-gather.16.cloned.1.call-start = ((), (), s32[]{:S(2)}) async-start(), calls=%async_computation.2 | async-start | bytes 1179648 | tf_op jit(solution)/shard_map/all_gather | solution.py:84
  8.7 214.7 %all-gather.12.cloned.1.call-start = ((), (), s32[]{:S(2)}) async-start(), calls=%async_computation | async-start | bytes 1179648 | tf_op jit(solution)/shard_map/all_gather | solution.py:101
  9.4 223.1 %all-gather.24.cloned.1.call-start = ((), (), s32[]{:S(2)}) async-start(), calls=%async_computation.6 | async-start | bytes 2621440 | tf_op jit(solution)/shard_map/all_gather | solution.py:119
  55.3 42.5 %copy-start.1 = (bf16[1024,128]{1,0:T(8,128)(2,1)S(1)}, bf16[1024,128]{1,0:T(8,128)(2,1)}, u32[]{:S(2)}) copy-start(bf16[1024,128]{1,0:T(8,128)(2,1)} %param.37) | copy-start | bytes 786436
  55.3 53.5 %copy-start.14 = (s32[4]{0:T(128)S(1)}, s32[4]{0:T(128)}, u32[]{:S(2)}) copy-start(s32[4]{0:T(128)} %param.24) | copy-start | bytes 52
  55.3 62.6 %copy-start.7 = (bf16[128,256]{1,0:T(8,128)(2,1)S(1)}, bf16[128,256]{1,0:T(8,128)(2,1)}, u32[]{:S(2)}) copy-start(bf16[128,256]{1,0:T(8,128)(2,1)} %param.32) | copy-start | bytes 196612
  55.4 100.0 %copy-start.5 = (f32[4,50,32]{1,2,0:T(8,128)S(1)}, f32[4,50,32]{1,2,0:T(8,128)}, u32[]{:S(2)}) copy-start(f32[4,50,32]{1,2,0:T(8,128)} %param.22) | copy-start | bytes 76804
  55.4 100.0 %copy-start.6 = (f32[4,50,32]{1,2,0:T(8,128)S(1)}, f32[4,50,32]{1,2,0:T(8,128)}, u32[]{:S(2)}) copy-start(f32[4,50,32]{1,2,0:T(8,128)} %param.23) | copy-start | bytes 76804
  55.4 179.6 %all-gather.26.cloned.1.call-start = ((), (), s32[]{:S(2)}) async-start(), calls=%async_computation.7 | async-start | bytes 2621440 | tf_op jit(solution)/shard_map/all_gather | solution.py:120
  96.4 68.9 %copy-start.9 = (f32[1024]{0:T(1024)S(1)}, f32[1024]{0:T(1024)}, u32[]{:S(2)}) copy-start(f32[1024]{0:T(1024)} %param.29) | copy-start | bytes 12292
  96.5 141.0 %all-gather.18.cloned.1.call-start = ((), (), s32[]{:S(2)}) async-start(), calls=%async_computation.3 | async-start | bytes 1179648 | tf_op jit(solution)/shard_map/all_gather | solution.py:131
  97.0 113.1 %copy-start.13 = (u32[32]{0:T(128)S(1)}, u32[32]{0:T(128)}, u32[]{:S(2)}) copy-start(u32[32]{0:T(128)} %constant.93) | copy-start | bytes 388
  97.0 114.3 %copy-start.12 = (s32[4]{0:T(128)S(1)}, s32[4]{0:T(128)}, u32[]{:S(2)}) copy-start(s32[4]{0:T(128)} %param.21) | copy-start | bytes 52
  97.1 183.2 %all-gather.20.cloned.1.call-start = ((), (), s32[]{:S(2)}) async-start(), calls=%async_computation.4 | async-start | bytes 2359296 | tf_op jit(solution)/shard_map/all_gather | solution.py:133
  97.8 232.3 %all-gather.22.cloned.1.call-start = ((), (), s32[]{:S(2)}) async-start(), calls=%async_computation.5 | async-start | bytes 2359296 | tf_op jit(solution)/shard_map/all_gather | solution.py:134
  97.9 7.8 %collective-permute-start = (bf16[1024,128]{1,0:T(8,128)(2,1)S(1)}, bf16[1024,128]{1,0:T(8,128)(2,1)S(1)}, u32[]{:S(2)}, u32[]{:S(2)}) collective-permute-start(bf16[1024,128]{1,0:T(8,128)(2,1)S(1)} %copy-done.1), channel_id=1, source_target_pairs={{0,4},{4,8},{8,12},{12,16},{16,20},{20,24},{24,28},{28,0},{1,5},{5... | collective-permute-start | bytes 786440 | tf_op jit(solution)/shard_map/ppermute | solution.py:138
  105.7 8.7 %collective-permute-start.1 = (bf16[1024,128]{1,0:T(8,128)(2,1)S(1)}, bf16[1024,128]{1,0:T(8,128)(2,1)S(1)}, u32[]{:S(2)}, u32[]{:S(2)}) collective-permute-start(bf16[1024,128]{1,0:T(8,128)(2,1)S(1)} %collective-permute-done), channel_id=1, source_target_pairs={{0,4},{4,8},{8,12},{12,16},{16,20},{20,24},{24,28},{28,0},{1,5},{5... | collective-permute-start | bytes 786440 | tf_op jit(solution)/shard_map/ppermute | solution.py:138
  114.4 37.7 %collective-permute-start.2 = (bf16[1024,128]{1,0:T(8,128)(2,1)S(1)}, bf16[1024,128]{1,0:T(8,128)(2,1)S(1)}, u32[]{:S(2)}, u32[]{:S(2)}) collective-permute-start(bf16[1024,128]{1,0:T(8,128)(2,1)S(1)} %collective-permute-done.1), channel_id=1, source_target_pairs={{0,4},{4,8},{8,12},{12,16},{16,20},{20,24},{24,28},{28,0},{1,5},{5... | collective-permute-start | bytes 786440 | tf_op jit(solution)/shard_map/ppermute | solution.py:138
  152.1 13.1 %copy-start.2 = (bf16[1024,128]{1,0:T(8,128)(2,1)}, bf16[1024,128]{1,0:T(8,128)(2,1)S(1)}, u32[]{:S(2)}) copy-start(bf16[1024,128]{1,0:T(8,128)(2,1)S(1)} %collective-permute-done.2) | copy-start | bytes 786436
  152.1 9.6 %collective-permute-start.3 = (bf16[1024,128]{1,0:T(8,128)(2,1)S(1)}, bf16[1024,128]{1,0:T(8,128)(2,1)}, u32[]{:S(2)}, u32[]{:S(2)}) collective-permute-start(bf16[1024,128]{1,0:T(8,128)(2,1)S(1)} %collective-permute-done.2), channel_id=1, source_target_pairs={{0,4},{4,8},{8,12},{12,16},{16,20},{20,24},{24,28},{28,0},{1,5},{5... | collective-permute-start | bytes 786440 | tf_op jit(solution)/shard_map/ppermute | solution.py:138
  161.6 9.4 %collective-permute-start.4 = (bf16[1024,128]{1,0:T(8,128)(2,1)}, bf16[1024,128]{1,0:T(8,128)(2,1)}, u32[]{:S(2)}, u32[]{:S(2)}) collective-permute-start(bf16[1024,128]{1,0:T(8,128)(2,1)} %collective-permute-done.3), channel_id=1, source_target_pairs={{0,4},{4,8},{8,12},{12,16},{16,20},{20,24},{24,28},{28,0},{1,5},{5... | collective-permute-start | bytes 786440 | tf_op jit(solution)/shard_map/ppermute | solution.py:138
  165.3 55.1 %copy-start.3 = (bf16[1024,128]{1,0:T(8,128)(2,1)S(1)}, bf16[1024,128]{1,0:T(8,128)(2,1)}, u32[]{:S(2)}) copy-start(bf16[1024,128]{1,0:T(8,128)(2,1)} %copy-done.2) | copy-start | bytes 786436
  171.0 36.8 %collective-permute-start.5 = (bf16[1024,128]{1,0:T(8,128)(2,1)}, bf16[1024,128]{1,0:T(8,128)(2,1)S(1)}, u32[]{:S(2)}, u32[]{:S(2)}) collective-permute-start(bf16[1024,128]{1,0:T(8,128)(2,1)} %collective-permute-done.4), channel_id=1, source_target_pairs={{0,4},{4,8},{8,12},{12,16},{16,20},{20,24},{24,28},{28,0},{1,5},{5... | collective-permute-start | bytes 786440 | tf_op jit(solution)/shard_map/ppermute | solution.py:138
  207.8 7.6 %collective-permute-start.6 = (bf16[1024,128]{1,0:T(8,128)(2,1)S(1)}, bf16[1024,128]{1,0:T(8,128)(2,1)S(1)}, u32[]{:S(2)}, u32[]{:S(2)}) collective-permute-start(bf16[1024,128]{1,0:T(8,128)(2,1)S(1)} %collective-permute-done.5), channel_id=1, source_target_pairs={{0,4},{4,8},{8,12},{12,16},{16,20},{20,24},{24,28},{28,0},{1,5},{5... | collective-permute-start | bytes 786440 | tf_op jit(solution)/shard_map/ppermute | solution.py:138
  231.5 5.6 %copy-start.4 = (bf16[4,50,256]{2,1,0:T(8,128)(2,1)S(1)}, bf16[4,50,256]{2,1,0:T(8,128)(2,1)}, u32[]{:S(2)}) copy-start(bf16[4,50,256]{2,1,0:T(8,128)(2,1)} %reshape.120) | copy-start | bytes 307204
  235.0 19.3 %copy-start.10 = (f32[1024]{0:T(1024)S(1)}, f32[1024]{0:T(1024)}, u32[]{:S(2)}) copy-start(f32[1024]{0:T(1024)} %param.34) | copy-start | bytes 12292
  248.5 5.4 %collective-permute-start.7 = (bf16[18,1024]{1,0:T(8,128)(2,1)S(1)}, bf16[18,1024]{1,0:T(8,128)(2,1)S(1)}, u32[]{:S(2)}, u32[]{:S(2)}) collective-permute-start(bf16[18,1024]{1,0:T(8,128)(2,1)S(1)} %slice), channel_id=1, source_target_pairs={{0,1},{1,2},{2,3},{4,5},{5,6},{6,7},{8,9},{9,10},{10,11},{12,13},{... | collective-permute-start | bytes 110600
  282.5 66.1 %copy-start.8 = (bf16[1024,32]{0,1:T(8,128)(2,1)S(1)}, bf16[1024,32]{0,1:T(8,128)(2,1)}, u32[]{:S(2)}) copy-start(bf16[1024,32]{0,1:T(8,128)(2,1)} %param.39) | copy-start | bytes 196612
  282.5 66.1 %copy-start.11 = (f32[1024]{0:T(1024)S(1)}, f32[1024]{0:T(1024)}, u32[]{:S(2)}) copy-start(f32[1024]{0:T(1024)} %param.38) | copy-start | bytes 12292
  342.7 5.4 %collective-permute-start.8 = (bf16[18,1024]{1,0:T(8,128)(2,1)S(1)}, bf16[18,1024]{1,0:T(8,128)(2,1)S(1)}, u32[]{:S(2)}, u32[]{:S(2)}) collective-permute-start(bf16[18,1024]{1,0:T(8,128)(2,1)S(1)} %slice.1), channel_id=1, source_target_pairs={{0,1},{1,2},{2,3},{4,5},{5,6},{6,7},{8,9},{9,10},{10,11},{12,13},{... | collective-permute-start | bytes 110600
Sparse Core Ops, SparseCore 0:
  10.1 40.5 all-gather.13
  52.8 38.9 all-gather.15
  94.0 44.5 all-gather.11
  139.9 22.9 all-gather.23
  164.4 22.5 all-gather.25
  188.9 40.5 all-gather.17
  231.6 48.7 all-gather.19
  282.4 47.6 all-gather.21
